TPU v7x, 32 devices: a whole 2x2x4 slice. The times are simulated.
32 devices in a mesh: dp: 4 (over y, x), mp: 8 (over z, core).
Axes of the slice: x: 2, y: 2, z: 4, core: 2. Of those that a mesh axis runs over, the one named last changes fastest.
Arguments:
- tokens: bfloat16 [4, 1024, 5120], P('dp', 'mp'), may hold values from -6 to 6
- ln_gain: float32 [5120], replicated, may hold values from 0.1 to 1.9
- ln_bias: float32 [5120], replicated, may hold values from -3 to 3
- w_qkv: bfloat16 [5120, 3, 4096], P(None, None, 'mp'), may hold values from -0.15625 to 0.15625
- w_out: bfloat16 [4096, 5120], P('mp'), may hold values from -0.09375 to 0.09375
- grad_partial: bfloat16 [4, 4096, 5120], P('dp', 'mp'), may hold values from -6 to 6
Outputs:
- mixed: bfloat16 [4, 1024, 5120], P('dp', 'mp')
- grad_sum: float32 [4096, 5120], P('mp')
All inputs are finite; a program needn't handle non-finite values.
Results may differ from a plain program's by a relative error of at most 0.014.
The roundings to bfloat16 on the way count: a program that leaves them out, or rounds other values in their place, can miss the bound.
Values may be sent and summed in bfloat16 or wider, within the bound.
A program may use at most 192 MiB of HBM per device.

v0:
```python
import jax
import jax.numpy as jnp
from jax import lax
from jax.sharding import PartitionSpec as P

HEAD = 128
SEQ = 128


def layer_norm(rows, ln_gain, ln_bias):
    values = rows.astype(jnp.float32)
    center = jnp.mean(values, axis=-1, keepdims=True)
    spread = jnp.mean((values - center) * (values - center), axis=-1, keepdims=True)
    return ((values - center) * lax.rsqrt(spread + 1e-06) * ln_gain + ln_bias).astype(jnp.bfloat16)


def body(tokens, ln_gain, ln_bias, w_qkv, w_out, grad_partial):
    local_rows = tokens[0]
    inner_dev = w_qkv.shape[2]
    heads_dev = inner_dev // HEAD
    weight_flat = w_qkv.reshape(w_qkv.shape[0], 3 * inner_dev)
    normed_local = layer_norm(local_rows, ln_gain, ln_bias)
    qkv = jnp.dot(
        lax.all_gather(normed_local, "mp", axis=0, tiled=True),
        weight_flat,
        preferred_element_type=jnp.float32,
    ).astype(jnp.bfloat16)
    images = qkv.shape[0] // SEQ
    query = qkv[:, :inner_dev].reshape(images, SEQ, heads_dev, HEAD)
    keys = qkv[:, inner_dev : 2 * inner_dev].reshape(images, SEQ, heads_dev, HEAD)
    values = qkv[:, 2 * inner_dev :].reshape(images, SEQ, heads_dev, HEAD)
    scores = jnp.einsum(
        "bqhd,bkhd->bhqk", query, keys, preferred_element_type=jnp.float32
    ) * HEAD ** (-0.5)
    scaled = scores - jnp.max(scores, axis=-1, keepdims=True)
    expsc = jnp.exp(scaled)
    attn = (expsc / jnp.sum(expsc, axis=-1, keepdims=True)).astype(jnp.bfloat16)
    context = jnp.einsum(
        "bhqk,bkhd->bqhd", attn, values, preferred_element_type=jnp.float32
    ).astype(jnp.bfloat16)
    context = context.reshape(images * SEQ, inner_dev)
    partial_sum = jnp.dot(context, w_out, preferred_element_type=jnp.float32).astype(jnp.bfloat16)
    partial_sum = lax.optimization_barrier(partial_sum)
    proj = lax.psum_scatter(
        partial_sum.astype(jnp.float32).astype(jnp.bfloat16), "mp", scatter_dimension=0, tiled=True
    ).astype(jnp.float32)
    mixed = (local_rows.astype(jnp.float32) + proj).astype(jnp.bfloat16)[None]
    grad_sum = lax.psum(grad_partial[0], "dp").astype(jnp.float32)
    return (mixed, grad_sum)


def solution(mesh):
    placed = (
        P("dp", "mp", None),
        P(),
        P(),
        P(None, None, "mp"),
        P("mp", None),
        P("dp", "mp", None),
    )
    return jax.shard_map(
        body,
        mesh=mesh,
        in_specs=placed,
        out_specs=(P("dp", "mp", None), P("mp", None)),
        check_vma=False,
    )
```

profile of v0, /device:TPU:0, one launch (start us, length us, event | category | flops | bytes accessed | tf_op | source)
XLA Modules:
  0.0 281.6 jit_solution(14720574091398433311)
XLA Ops:
  8.0 0.0 copy-start
  8.0 0.0 copy-start.3
  8.0 0.0 copy-start.2
  8.0 0.0 all-gather.2.cloned.1.call-start
  8.1 1.7 convert_reduce_fusion
  9.8 1.8 fusion.5
  11.6 0.0 copy-done
  11.6 0.0 copy-done.3
  11.6 0.0 copy-done.2
  11.6 1.6 fusion.8
  13.2 0.0 all-gather.2.cloned.1.call-update
  13.3 0.0 all-reduce.2.cloned.1.call-start
  13.3 0.5 all-reduce.2.cloned.1.call-update
  13.8 0.0 reduce-scatter.2.cloned.1.call-start
  13.9 21.1 %copy.12 = bf16[5120,3,512]{0,2,1:T(8,128)(2,1)} copy(bf16[5120,3,512]{2,0,1:T(8,128)(2,1)} %param.9) | data formatting | bytes 31457280 | tf_op args[3]
  35.0 80.5 %all-gather.2.cloned.1.call-done = bf16[1024,5120]{1,0:T(8,128)(2,1)} async-done(((bf16[128,5120]{1,0:T(8,128)(2,1)}), bf16[1024,5120]{1,0:T(8,128)(2,1)}) %all-gather.2.cloned.1.call-update) | async-done | bytes 10485776 | tf_op jit(solution)/shard_map/all_gather | solution.py:24
  115.5 23.1 %convolution_convert_fusion.1 = bf16[1024,1536]{1,0:T(8,128)(2,1)S(1)} fusion(bf16[1024,5120]{1,0:T(8,128)(2,1)} %all-gather.2.cloned.1.call-done, bf16[5120,1536]{0,1:T(8,128)(2,1)} %bitcast.38), kind=kOutput, calls=%fused_computation.2 | convolution fusion | flops 16107700224 | bytes 29360128 | tf_op jit(solution)/shard_map/dot_general | solution.py:23
  138.6 1.6 fusion.37
  140.2 1.3 reshape.38
  141.5 2.2 reshape.39
  143.7 1.1 reshape.37
  144.8 2.3 fusion.38
  147.1 0.0 copy-done.1
  147.1 2.2 fusion.16
  149.3 2.9 %fusion.11 = bf16[8,128,4,128]{1,3,2,0:T(8,128)(2,1)S(1)} fusion(bf16[8,128,4,128]{3,2,1,0:T(4,128)(2,1)} %reshape.37, f32[8,4,128]{2,1,0:T(4,128)S(1)} %fusion.38, f32[8,4,128,128]{2,3,1,0:T(8,128)} %fusion.16), kind=kOutput, calls=%fused_computation.19 | convolution fusion | flops 136843392 | bytes 4210688 | tf_op jit(solution)/shard_map/bhqk,bkhd->bqhd/dot_general | solution.py:38
  152.2 0.7 copy.17
  152.9 10.8 %convolution_convert_fusion = bf16[1024,5120]{1,0:T(8,128)(2,1)} fusion(bf16[512,5120]{1,0:T(8,128)(2,1)} %param.10, bf16[64,8,8,128]{3,2,1,0:T(8,128)(2,1)S(1)} %bitcast.40), kind=kOutput, calls=%fused_computation.1 | convolution fusion | flops 5373952000 | bytes 16777216 | tf_op jit(solution)/shard_map/dot_general | solution.py:42
  163.6 0.0 reduce-scatter.2.cloned.1.call-update
  163.7 0.0 all-reduce.2.cloned.1.call-done
  163.7 7.9 %convert_element_type.46 = f32[512,5120]{1,0:T(8,128)} convert(bf16[512,5120]{1,0:T(8,128)(2,1)} %all-reduce.2.cloned.1.call-done) | non-fusion elementwise | flops 2621440 | bytes 15728640 | tf_op jit(solution)/shard_map/convert_element_type | solution.py:48
  171.6 99.8 %reduce-scatter.2.cloned.1.call-done = bf16[128,5120]{1,0:T(8,128)(2,1)} async-done(((bf16[1024,5120]{1,0:T(8,128)(2,1)}), bf16[128,5120]{1,0:T(8,128)(2,1)}) %reduce-scatter.2.cloned.1.call-update) | async-done | bytes 1310736 | tf_op jit(solution)/shard_map/reduce_scatter | solution.py:44
  271.4 2.7 fusion.12
  (3 shorter events, 0.0 us)
Async XLA Ops:
  8.0 3.6 %copy-start = (bf16[1,128,5120]{2,1,0:T(8,128)(2,1)S(1)}, bf16[1,128,5120]{2,1,0:T(8,128)(2,1)}, u32[]{:S(2)}) copy-start(bf16[1,128,5120]{2,1,0:T(8,128)(2,1)} %param.6) | copy-start | bytes 3932164
  8.0 3.6 %copy-start.3 = (f32[5120]{0:T(1024)S(1)}, f32[5120]{0:T(1024)}, u32[]{:S(2)}) copy-start(f32[5120]{0:T(1024)} %param.7) | copy-start | bytes 61444
  8.0 3.6 %copy-start.2 = (f32[5120]{0:T(1024)S(1)}, f32[5120]{0:T(1024)}, u32[]{:S(2)}) copy-start(f32[5120]{0:T(1024)} %param.8) | copy-start | bytes 61444
  8.0 107.5 %all-gather.2.cloned.1.call-start = ((), (), s32[]{:S(2)}) async-start(), calls=%async_computation.1 | async-start | bytes 11796480 | tf_op jit(solution)/shard_map/all_gather | solution.py:24
  13.3 150.4 %all-reduce.2.cloned.1.call-start = ((), (), s32[]{:S(2)}) async-start(), calls=%async_computation.3 | async-start | bytes 10485760 | tf_op jit(solution)/shard_map/psum | solution.py:48
  13.8 257.6 %reduce-scatter.2.cloned.1.call-start = ((), (), s32[]{:S(2)}) async-start(), calls=%async_computation.2 | async-start | bytes 11796480 | tf_op jit(solution)/shard_map/reduce_scatter | solution.py:44
  144.8 2.3 copy-start.1
Sparse Core Ops, SparseCore 0:
  13.4 102.0 all-gather.1
  163.8 107.5 reduce-scatter.1
Sparse Core Ops, SparseCore 1:
  17.0 123.3 all-reduce.1
where the time goes:
time: 282 us
  waiting for transfers between devices  181 us (64%)
  matrix products  41.2 us (15%)
  local copies, waits for them, and re-layouts  27.9 us (10%)
  other arithmetic  15.8 us (6%)
  between operations  15.6 us (6%)
    reduce_scatter x1, waiting for transfers between devices, body(): lax.psum_scatter(partial_sum.astype(jnp.float32).astype(jnp.bfloat16), 'm...  99.8 us
    all_gather x1, waiting for transfers between devices, body(): lax.all_gather(normed_local, 'mp', axis=0, tiled=True)  80.5 us
    dot_general x1, matrix products, body(): jnp.dot(lax.all_gather(normed_local, 'mp', axis=0, tiled=True), weight_fl...  23.1 us
    unnamed x9, local copies, waits for them, and re-layouts  21.1 us
    dot_general x1, matrix products, body(): jnp.dot(context, w_out, preferred_element_type=jnp.float32)  10.8 us
    convert_element_type x1, other arithmetic, body(): grad_sum = lax.psum(grad_partial[0], 'dp').astype(jnp.float32)  7.93 us
  transfers between devices with their start and end apart: 3, of which 2 were waited for; matrix products, arithmetic and copies ran while one was open for 27% of the time, Pallas kernels for 0%

commit v1 on v0

v1 whole, which is shorter than its diff:
```python
import functools

import jax
import jax.numpy as jnp
from jax import lax
from jax.experimental import pallas as pl
from jax.experimental.pallas import tpu as pltpu
from jax.sharding import PartitionSpec as P

HEAD = 128
SEQ = 128
TILE = 256
PIECES = 4
MESH = pl.DeviceIdType.MESH


def layer_norm(rows, ln_gain, ln_bias):
    values = rows.astype(jnp.float32)
    center = jnp.mean(values, axis=-1, keepdims=True)
    spread = jnp.mean((values - center) * (values - center), axis=-1, keepdims=True)
    return ((values - center) * lax.rsqrt(spread + 1e-06) * ln_gain + ln_bias).astype(jnp.bfloat16)


def kernel(
    n,
    normed,
    tokens,
    wq_hbm,
    wo_hbm,
    out,
    wq,
    wo,
    blocks,
    part,
    theirs,
    chain,
    qkv,
    ctx,
    load_sem,
    up_send,
    up_recv,
    dn_send,
    dn_recv,
    pr_send,
    pr_recv,
    pp_send,
    pp_recv,
    cu_send,
    cu_recv,
    cd_send,
    cd_recv,
):
    chips = n // 2
    me = lax.axis_index("mp")
    c = me // 2
    s = me % 2
    mate = c * 2 + 1 - s
    above = me + 2
    below = me - 2
    up = jnp.minimum(chips - 1 - c, 1)
    dn = jnp.minimum(c, 1)
    has_up = up > 0
    has_dn = dn > 0
    rows, width = normed.shape
    inner = wo_hbm.shape[0]
    wide = width // PIECES

    def remote(src, dst, send, recv, target):
        return pltpu.make_async_remote_copy(
            src_ref=src,
            dst_ref=dst,
            send_sem=send,
            recv_sem=recv,
            device_id={"mp": target},
            device_id_type=MESH,
        )

    load_q = pltpu.make_async_copy(wq_hbm, wq, load_sem.at[0])
    load_o = pltpu.make_async_copy(wo_hbm, wo, load_sem.at[1])
    load_x = pltpu.make_async_copy(normed, blocks.at[me], load_sem.at[2])
    load_q.start()
    load_o.start()
    load_x.start()

    barrier = pltpu.get_barrier_semaphore()
    pl.semaphore_signal(barrier, inc=1, device_id={"mp": mate}, device_id_type=MESH)

    @pl.when(has_up)
    def _():
        pl.semaphore_signal(barrier, inc=1, device_id={"mp": above}, device_id_type=MESH)

    @pl.when(has_dn)
    def _():
        pl.semaphore_signal(barrier, inc=1, device_id={"mp": below}, device_id_type=MESH)

    pl.semaphore_wait(barrier, 1 + up + dn)

    def block_up(src, slot, d):
        return remote(src, blocks.at[slot], up_send.at[d], up_recv.at[d], above)

    def block_dn(src, slot, d):
        return remote(src, blocks.at[slot], dn_send.at[d], dn_recv.at[d], below)

    def block_mate(src, slot, d, k):
        return remote(src, blocks.at[slot], pr_send.at[d, k], pr_recv.at[d, k], mate)

    def share_mate(slot, d, k):
        return remote(blocks.at[slot], theirs.at[k], pp_send.at[d, k], pp_recv.at[d, k], mate)

    def cols(q):
        return slice(q * wide, (q + 1) * wide)

    def sum_up(t, q):
        return remote(
            part.at[t, :, cols(q)], chain.at[t, :, cols(q)], cu_send.at[t, q], cu_recv.at[t, q], above
        )

    def sum_dn(t, q):
        slot = jnp.where(t == c - 1, chips, t)
        return remote(
            part.at[t, :, cols(q)], chain.at[slot, :, cols(q)], cd_send.at[t, q], cd_recv.at[t, q], below
        )

    @pl.when(has_up)
    def _():
        block_up(normed, me, 0).start()

    @pl.when(has_dn)
    def _():
        block_dn(normed, me, 0).start()

    block_mate(normed, me, 0, 0).start()
    load_x.wait()
    load_q.wait()
    load_o.wait()

    per_part = inner // TILE

    def attend(slot):
        def project(j, carry):
            which = j // per_part
            at = pl.multiple_of((j % per_part) * TILE, TILE)
            product = jnp.dot(
                blocks[slot], wq[which, :, pl.ds(at, TILE)], preferred_element_type=jnp.float32
            )
            qkv[which, :, pl.ds(at, TILE)] = product.astype(jnp.bfloat16)
            return carry

        lax.fori_loop(0, 3 * per_part, project, 0)
        for image in range(rows // SEQ):
            here = slice(image * SEQ, (image + 1) * SEQ)
            for h in range(inner // HEAD):
                lanes = slice(h * HEAD, (h + 1) * HEAD)
                scores = lax.dot_general(
                    qkv[0, here, lanes],
                    qkv[1, here, lanes],
                    (((1,), (1,)), ((), ())),
                    preferred_element_type=jnp.float32,
                ) * HEAD ** (-0.5)
                expsc = jnp.exp(scores - jnp.max(scores, axis=-1, keepdims=True))
                attn = (expsc / jnp.sum(expsc, axis=-1, keepdims=True)).astype(jnp.bfloat16)
                ctx[here, lanes] = jnp.dot(
                    attn, qkv[2, here, lanes], preferred_element_type=jnp.float32
                ).astype(jnp.bfloat16)

    def output(at):
        return jnp.dot(
            ctx[...], wo[:, pl.ds(at, TILE)], preferred_element_type=jnp.float32
        ).astype(jnp.bfloat16)

    def chain_step(e):
        @pl.when(dn * jnp.maximum(e - c, 0) > 0)
        def _():
            for q in range(PIECES):
                sum_up(e, q).wait_recv()
                part[e, :, cols(q)] = (
                    part[e, :, cols(q)].astype(jnp.float32) + chain[e, :, cols(q)].astype(jnp.float32)
                ).astype(jnp.bfloat16)
                sum_up(e, q).start()

        t = chips - 1 - e

        @pl.when(up * jnp.maximum(c - t, 0) > 0)
        def _():
            for q in range(PIECES):
                remote(
                    part.at[t, :, cols(q)],
                    chain.at[t, :, cols(q)],
                    cd_send.at[t, q],
                    cd_recv.at[t, q],
                    below,
                ).wait_recv()
                part[t, :, cols(q)] = (
                    part[t, :, cols(q)].astype(jnp.float32) + chain[t, :, cols(q)].astype(jnp.float32)
                ).astype(jnp.bfloat16)
                sum_dn(t, q).start()

    def step(d, carry):
        lo = c - d
        hi = c + d
        lo_ok = jnp.minimum(jnp.maximum(lo + 1, 0), 1)
        hi_ok = jnp.minimum(jnp.maximum(chips - hi, 0), jnp.minimum(d, 1))

        @pl.when(lo_ok * d > 0)
        def _():
            slot = lo * 2 + s
            block_up(blocks.at[slot], slot, d - 1).wait_recv()

            @pl.when(up + d * 0 > 0)
            def _():
                block_up(blocks.at[slot], slot, d).start()

            block_mate(blocks.at[slot], slot, d, 0).start()

        @pl.when(hi_ok > 0)
        def _():
            slot = hi * 2 + s
            block_dn(blocks.at[slot], slot, d - 1).wait_recv()

            @pl.when(dn + d * 0 > 0)
            def _():
                block_dn(blocks.at[slot], slot, d).start()

            block_mate(blocks.at[slot], slot, d, 1).start()

        def one(i, inner_carry):
            k = i % 2
            own = i // 2
            t = jnp.where(k == 0, lo, hi)

            @pl.when(jnp.where(k == 0, lo_ok, hi_ok) > 0)
            def _():
                slot = t * 2 + jnp.where(own == 1, s, 1 - s)

                @pl.when(own == 0)
                def _():
                    block_mate(blocks.at[slot], slot, d, k).wait_recv()

                attend(slot)

                @pl.when(own == 0)
                def _():
                    def put(j, inside):
                        at = pl.multiple_of(j * TILE, TILE)
                        blocks[slot, :, pl.ds(at, TILE)] = output(at)
                        return inside

                    lax.fori_loop(0, width // TILE, put, 0)
                    share_mate(slot, d, k).start()

                @pl.when(own == 1)
                def _():
                    share_mate(slot, d, k).wait_recv()

                    def put(j, inside):
                        at = pl.multiple_of(j * TILE, TILE)
                        both = output(at).astype(jnp.float32) + theirs[k, :, pl.ds(at, TILE)].astype(
                            jnp.float32
                        )
                        part[t, :, pl.ds(at, TILE)] = both.astype(jnp.bfloat16)
                        return inside

                    lax.fori_loop(0, width // TILE, put, 0)

                    @pl.when((1 - dn) * t > 0)
                    def _():
                        for q in range(PIECES):
                            sum_up(t, q).start()

                    @pl.when((1 - up) * (chips - 1 - t) > 0)
                    def _():
                        for q in range(PIECES):
                            sum_dn(t, q).start()

            return inner_carry

        lax.fori_loop(0, 4, one, 0)

        @pl.when(d >= 2)
        def _():
            chain_step(d - 1)

        return carry

    lax.fori_loop(0, chips, step, 0)
    if chips > 1:
        chain_step(chips - 1)

    @pl.when(has_up)
    def _():
        for q in range(PIECES):
            remote(
                part.at[c, :, cols(q)],
                chain.at[chips, :, cols(q)],
                cd_send.at[c, q],
                cd_recv.at[c, q],
                below,
            ).wait_recv()

    @pl.when(has_dn)
    def _():
        for q in range(PIECES):
            sum_up(c, q).wait_recv()

    def total(from_dn, from_up):
        for q in range(PIECES):
            value = part[c, :, cols(q)].astype(jnp.float32)
            if from_dn:
                value = value + chain[c, :, cols(q)].astype(jnp.float32)
            if from_up:
                value = value + chain[chips, :, cols(q)].astype(jnp.float32)
            out[:, cols(q)] = (tokens[:, cols(q)].astype(jnp.float32) + value).astype(jnp.bfloat16)

    @pl.when(dn * up > 0)
    def _():
        total(True, True)

    @pl.when(dn * (1 - up) > 0)
    def _():
        total(True, False)

    @pl.when((1 - dn) * up > 0)
    def _():
        total(False, True)

    @pl.when((1 - dn) * (1 - up) > 0)
    def _():
        total(False, False)

    def drain(d, carry):
        hi_ok = jnp.minimum(jnp.maximum(chips - c - d, 0), jnp.minimum(d, 1))

        @pl.when(c - d >= 0)
        def _():
            slot = (c - d) * 2 + s
            other = (c - d) * 2 + 1 - s

            @pl.when(up + d * 0 > 0)
            def _():
                block_up(blocks.at[slot], slot, d).wait_send()

            block_mate(blocks.at[slot], slot, d, 0).wait_send()
            share_mate(other, d, 0).wait_send()

        @pl.when(jnp.maximum(chips - c - d, 0) * dn > 0)
        def _():
            slot = (c + d) * 2 + s
            block_dn(blocks.at[slot], slot, d).wait_send()

        @pl.when(hi_ok > 0)
        def _():
            slot = (c + d) * 2 + s
            other = (c + d) * 2 + 1 - s
            block_mate(blocks.at[slot], slot, d, 1).wait_send()
            share_mate(other, d, 1).wait_send()

        @pl.when(d > c)
        def _():
            for q in range(PIECES):
                sum_up(d, q).wait_send()

        @pl.when(d < c)
        def _():
            for q in range(PIECES):
                sum_dn(d, q).wait_send()

        return carry

    lax.fori_loop(0, chips, drain, 0)


def body(n, tokens, ln_gain, ln_bias, w_qkv, w_out, grad_partial):
    local_rows = tokens[0]
    rows, width = local_rows.shape
    inner = w_out.shape[0]
    chips = n // 2
    normed = layer_norm(local_rows, ln_gain, ln_bias)
    dma = pltpu.SemaphoreType.DMA
    flops = 2 * rows * n * width * inner * 4
    mixed = pl.pallas_call(
        functools.partial(kernel, n),
        out_shape=jax.ShapeDtypeStruct((rows, width), jnp.bfloat16),
        in_specs=[
            pl.BlockSpec(memory_space=pl.ANY),
            pl.BlockSpec(memory_space=pltpu.VMEM),
            pl.BlockSpec(memory_space=pl.ANY),
            pl.BlockSpec(memory_space=pl.ANY),
        ],
        out_specs=pl.BlockSpec(memory_space=pltpu.VMEM),
        scratch_shapes=[
            pltpu.VMEM((3, width, inner), jnp.bfloat16),
            pltpu.VMEM((inner, width), jnp.bfloat16),
            pltpu.VMEM((n, rows, width), jnp.bfloat16),
            pltpu.VMEM((chips, rows, width), jnp.bfloat16),
            pltpu.VMEM((2, rows, width), jnp.bfloat16),
            pltpu.VMEM((chips + 1, rows, width), jnp.bfloat16),
            pltpu.VMEM((3, rows, inner), jnp.bfloat16),
            pltpu.VMEM((rows, inner), jnp.bfloat16),
            dma((3,)),
            dma((chips,)),
            dma((chips,)),
            dma((chips,)),
            dma((chips,)),
            dma((chips, 2)),
            dma((chips, 2)),
            dma((chips, 2)),
            dma((chips, 2)),
            dma((chips, PIECES)),
            dma((chips, PIECES)),
            dma((chips, PIECES)),
            dma((chips, PIECES)),
        ],
        compiler_params=pltpu.CompilerParams(
            collective_id=0, has_side_effects=True, vmem_limit_bytes=66_000_000
        ),
        cost_estimate=pl.CostEstimate(
            flops=flops * 8, bytes_accessed=300_000_000, transcendentals=0
        ),
    )(normed, local_rows, jnp.transpose(w_qkv, (1, 0, 2)), w_out)[None]
    grad_sum = lax.psum(grad_partial[0], "dp").astype(jnp.float32)
    return (mixed, grad_sum)


def solution(mesh):
    placed = (
        P("dp", "mp", None),
        P(),
        P(),
        P(None, None, "mp"),
        P("mp", None),
        P("dp", "mp", None),
    )
    return jax.shard_map(
        functools.partial(body, mesh.shape["mp"]),
        mesh=mesh,
        in_specs=placed,
        out_specs=(P("dp", "mp", None), P("mp", None)),
        check_vma=False,
    )
```

time: 282 us -> 225 us (0.80)
  Pallas kernels: 0 us -> 198 us
  waiting for transfers between devices: 181 us -> 0.69 us
  matrix products: 41.2 us -> 0 us
  local copies, waits for them, and re-layouts: 27.9 us -> 1.7 us
  other arithmetic: 15.8 us -> 10.4 us
    pallas_call x0 -> x1, Pallas kernels: none -> 198 us  [body(): pl.pallas_call(functools.partial(kernel, n), out_shape=jax.ShapeDtypeStru...]
    reduce_scatter x1 -> x0, waiting for transfers between devices: 99.8 us -> none  [body(): lax.psum_scatter(partial_sum.astype(jnp.float32).astype(jnp.bfloat16), 'm...]
    all_gather x1 -> x0, waiting for transfers between devices: 80.5 us -> none  [body(): lax.all_gather(normed_local, 'mp', axis=0, tiled=True)]
    dot_general x4 -> x0, matrix products: 38.9 us -> none  [the longest x1 23.1 us: body(): jnp.dot(lax.all_gather(normed_local, 'mp', axis=0, tiled=True), weight_fl...]
    unnamed x9, local copies, waits for them, and re-layouts: 21.1 us -> 1.7 us
    reshape x3 -> x0, local copies, waits for them, and re-layouts: 4.59 us -> none  [the longest x1 2.16 us: body(): keys = qkv[:, inner_dev:2 * inner_dev].reshape(images, SEQ, heads_dev, HEAD)]
  transfers between devices with their start and end apart: 3 -> 1, of which waited for: 2 -> 0; matrix products, arithmetic and copies ran while one was open for 27% -> 1% of each run, Pallas kernels for 0% -> 88%
where the time goes in v1:
time: 225 us
  Pallas kernels  198 us (88%)
  between operations  14.1 us (6%)
  other arithmetic  10.4 us (5%)
    pallas_call x1, Pallas kernels, body(): pl.pallas_call(functools.partial(kernel, n), out_shape=jax.ShapeDtypeStru...  198 us
    convert_element_type x1, other arithmetic, body(): grad_sum = lax.psum(grad_partial[0], 'dp').astype(jnp.float32)  8.03 us
  transfers between devices with their start and end apart: 1, of which 0 were waited for; matrix products, arithmetic and copies ran while one was open for 1% of the time, Pallas kernels for 88%

profile of v1, /device:TPU:0, one launch (start us, length us, event | category | flops | bytes accessed | tf_op | source)
XLA Modules:
  0.0 225.2 jit_solution(649097263252124873)
XLA Ops:
  7.2 0.0 all-reduce.2.cloned.1.call-start
  7.2 0.0 copy-start
  7.2 0.7 all-reduce.2.cloned.1.call-update
  7.9 0.6 copy-done
  8.5 0.0 copy-start.2
  8.5 0.0 copy-start.3
  8.5 0.3 convert_reduce_fusion
  8.8 0.5 fusion.2
  9.3 0.0 copy-done.2
  9.3 0.0 copy-done.3
  9.3 1.6 fusion.5.normed
  11.0 198.3 %shard_map.77 = bf16[128,5120]{1,0:T(8,128)(2,1)} custom-call(bf16[128,5120]{1,0:T(8,128)(2,1)} %fusion.5.normed, bf16[128,5120]{1,0:T(8,128)(2,1)} %bitcast.7, bf16[3,5120,512]{2,1,0:T(8,128)(2,1)} %bitcast.10, bf16[512,5120]{1,0:T(8,128)(2,1)} %wo_hbm.1), custom_call_target="tpu_custom_call" | custom-call | flops 171798691840 | bytes 300000000 | tf_op jit(solution)/shard_map/pallas_call | solution.py:380
  209.2 0.0 copy-start.1
  209.2 0.0 all-reduce.2.cloned.1.call-done
  209.3 8.0 %convert_element_type.11 = f32[512,5120]{1,0:T(8,128)} convert(bf16[512,5120]{1,0:T(8,128)(2,1)} %all-reduce.2.cloned.1.call-done) | non-fusion elementwise | flops 2621440 | bytes 15728640 | tf_op jit(solution)/shard_map/convert_element_type | solution.py:420
  217.3 0.0 copy-done.1
  217.3 1.1 copy.11
  (2 shorter events, 0.0 us)
Async XLA Ops:
  7.2 202.1 %all-reduce.2.cloned.1.call-start = ((), (), s32[]{:S(2)}) async-start(), calls=%async_computation | async-start | bytes 10485760 | tf_op jit(solution)/shard_map/psum | solution.py:420
  7.2 1.3 copy-start
  8.5 0.8 copy-start.2
  8.5 0.8 copy-start.3
  209.2 8.1 %copy-start.1 = (bf16[128,5120]{1,0:T(8,128)(2,1)S(1)}, bf16[128,5120]{1,0:T(8,128)(2,1)}, u32[]{:S(2)}) copy-start(bf16[128,5120]{1,0:T(8,128)(2,1)} %shard_map.77) | copy-start | bytes 3932164
Sparse Core Ops, SparseCore 0:
  11.3 123.7 all-reduce.1
